TPU v7x, 16 devices: a 4x2x1 block of a 4x4x8 slice. The times are simulated.
16 devices in a mesh: dp: 4 (over y, z, core), tp: 4 (over x).
Axes of the slice: x: 4, y: 2, z: 1, core: 2. Of those that a mesh axis runs over, the one named last changes fastest.
The devices are a block of a 4x4x8 slice.
Arguments:
- x: bfloat16 [3584, 5120], P(('dp', 'tp')), parts along dimension 0
- w_gate: bfloat16 [5120, 12288], P(None, 'tp')
- w_up: bfloat16 [5120, 12288], P(None, 'tp')
- w_down: bfloat16 [12288, 5120], P('tp')
Outputs:
- output: bfloat16 [3584, 5120], P(('dp', 'tp')), parts along dimension 0
There are 4 independent parts. A program takes and returns all parts, laid end to end along the dimension named above; an argument that names none is the same for every part.
All inputs are finite; a program needn't handle non-finite values.
Results may differ from a plain program's by a relative error of at most 0.016.
Values are sent between devices in bfloat16 or wider.
A program may use at most 768 MiB of HBM per device.

v0:
```python
import jax
import jax.numpy as jnp
from jax import lax
from jax.sharding import PartitionSpec as P


def solution(mesh):
    def step(x, w_gate, w_up, w_down):
        rows = lax.all_gather(x, "tp", axis=0, tiled=True)
        gate = jnp.dot(rows, w_gate, preferred_element_type=jnp.float32)
        up = jnp.dot(rows, w_up, preferred_element_type=jnp.float32)
        hidden = (jax.nn.silu(gate) * up).astype(jnp.bfloat16)
        term = jnp.dot(hidden, w_down, preferred_element_type=jnp.float32).astype(jnp.bfloat16)
        return lax.psum_scatter(term, "tp", scatter_dimension=0, tiled=True)

    return jax.shard_map(
        step,
        mesh=mesh,
        in_specs=(P(("dp", "tp"), None), P(None, "tp"), P(None, "tp"), P("tp", None)),
        out_specs=P(("dp", "tp"), None),
        check_vma=False,
    )
```

profile of v0, /device:TPU:112, one launch (start us, length us, event | category | flops | bytes accessed | tf_op | source)
XLA Modules:
  0.0 291.8 jit_solution(16240867615743924404)
XLA Ops:
  6.5 0.0 all-gather.2.cloned.1.call-start
  6.6 0.7 all-gather.2.cloned.1.call-update
  7.3 0.1 reduce-scatter.2.cloned.1.call-start
  7.4 90.4 %all-gather.2.cloned.1.call-done = bf16[896,5120]{1,0:T(8,128)(2,1)} async-done(((bf16[224,5120]{1,0:T(8,128)(2,1)}), bf16[896,5120]{1,0:T(8,128)(2,1)}) %all-gather.2.cloned.1.call-update) | async-done | bytes 9175056 | tf_op jit(solution)/shard_map/all_gather | solution.py:9
  97.7 0.0 copy-start
  97.7 33.8 %fusion = f32[896,3072]{1,0:T(8,128)S(1)} fusion(bf16[896,5120]{1,0:T(8,128)(2,1)} %all-gather.2.cloned.1.call-done, bf16[5120,3072]{1,0:T(8,128)(2,1)} %param.5), kind=kOutput, calls=%fused_computation.2 | convolution fusion | flops 28185722880 | bytes 51642368 | tf_op jit(solution)/shard_map/dot_general | solution.py:10
  131.5 0.0 copy-done
  131.5 34.5 %multiply_convert_fusion = bf16[896,3072]{1,0:T(8,128)(2,1)} fusion(f32[896,3072]{1,0:T(8,128)S(1)} %fusion, bf16[896,5120]{1,0:T(8,128)(2,1)S(1)} %copy-done, bf16[5120,3072]{1,0:T(8,128)(2,1)} %param.6), kind=kOutput, calls=%fused_computation | convolution fusion | flops 28202237952 | bytes 57147392 | tf_op jit(solution)/shard_map/dot_general | solution.py:11
  166.0 35.0 %convolution_convert_fusion = bf16[896,5120]{1,0:T(8,128)(2,1)} fusion(bf16[896,3072]{1,0:T(8,128)(2,1)} %multiply_convert_fusion, bf16[3072,5120]{1,0:T(8,128)(2,1)} %param.7), kind=kOutput, calls=%fused_computation.1 | convolution fusion | flops 28190310400 | bytes 46137344 | tf_op jit(solution)/shard_map/dot_general | solution.py:13
  201.0 0.1 reduce-scatter.2.cloned.1.call-update
  201.0 83.9 %reduce-scatter.2.cloned.1.call-done = bf16[224,5120]{1,0:T(8,128)(2,1)} async-done(((bf16[896,5120]{1,0:T(8,128)(2,1)}), bf16[224,5120]{1,0:T(8,128)(2,1)}) %reduce-scatter.2.cloned.1.call-update) | async-done | bytes 2293776 | tf_op jit(solution)/shard_map/reduce_scatter | solution.py:14
Async XLA Ops:
  6.5 91.2 %all-gather.2.cloned.1.call-start = ((), (), s32[]{:S(2)}) async-start(), calls=%async_computation.1 | async-start | bytes 11468800 | tf_op jit(solution)/shard_map/all_gather | solution.py:9
  7.3 277.7 %reduce-scatter.2.cloned.1.call-start = ((), (), s32[]{:S(2)}) async-start(), calls=%async_computation.2 | async-start | bytes 11468800 | tf_op jit(solution)/shard_map/reduce_scatter | solution.py:14
  97.7 33.8 %copy-start = (bf16[896,5120]{1,0:T(8,128)(2,1)S(1)}, bf16[896,5120]{1,0:T(8,128)(2,1)}, u32[]{:S(2)}) copy-start(bf16[896,5120]{1,0:T(8,128)(2,1)} %all-gather.2.cloned.1.call-done) | copy-start | bytes 27525124
Sparse Core Ops, SparseCore 0:
  8.9 88.7 all-gather.1
  201.2 83.7 reduce-scatter.1
where the time goes:
time: 292 us
  waiting for transfers between devices  175 us (60%)
  matrix products  103 us (35%)
  between operations  13.4 us (5%)
    all_gather x1, waiting for transfers between devices, step(): rows = lax.all_gather(x, 'tp', axis=0, tiled=True)  90.4 us
    reduce_scatter x1, waiting for transfers between devices, step(): return lax.psum_scatter(term, 'tp', scatter_dimension=0, tiled=True)  83.9 us
    dot_general x1, matrix products, step(): jnp.dot(hidden, w_down, preferred_element_type=jnp.float32)  35 us
    dot_general x1, matrix products, step(): up = jnp.dot(rows, w_up, preferred_element_type=jnp.float32)  34.5 us
    dot_general x1, matrix products, step(): gate = jnp.dot(rows, w_gate, preferred_element_type=jnp.float32)  33.8 us
  transfers between devices with their start and end apart: 2, of which 2 were waited for; matrix products, arithmetic and copies ran while one was open for 0% of the time, Pallas kernels for 0%

commit v1 on v0

v1 whole, which is shorter than its diff:
```python
import functools

import jax
import jax.numpy as jnp
from jax import lax
from jax.experimental import pallas as pl
from jax.experimental.pallas import tpu as pltpu
from jax.sharding import PartitionSpec as P

HALVES = 2
KC = 512
NT = 1536
AHEAD = 3


def when(cond, f):
    if isinstance(cond, bool):
        if cond:
            f()
    else:
        pl.when(cond)(f)


def kernel(
    n, x, wg, wu, wd, y,
    xg, accg, accu, hid, wgu, wdb, pout, pin, qout, qin, tq, own, yst,
    ld_sem, w_sem, wd_sem, own_send, own_recv, fwd_send, fwd_recv,
    p_send, p_recv, q_send, q_recv, y_sem,
):
    me = lax.axis_index("tp")
    right, left = lax.rem(me + 1, n), lax.rem(me + n - 1, n)
    target = (right, left)
    rows, cols = x.shape
    part = rows // HALVES
    chunks = cols // KC
    total = HALVES * chunks
    hidden = wg.shape[1]
    half = KC // 2
    slot = [pl.ds(i * part, part) for i in range(n)]
    side = (pl.ds(0, half), pl.ds(half, half))

    def load(g):
        h, c = g // chunks, g % chunks
        return pltpu.make_async_copy(
            x.at[pl.ds(pl.multiple_of(h * part, part), part), pl.ds(pl.multiple_of(c * KC, KC), KC)],
            xg.at[g, slot[0]],
            ld_sem.at[g],
        )

    def remote(d, src, dst, send, recv):
        return pltpu.make_async_remote_copy(
            src_ref=src, dst_ref=dst, send_sem=send, recv_sem=recv,
            device_id={"tp": target[d]}, device_id_type=pl.DeviceIdType.MESH,
        )

    def own_copy(d, g):
        return remote(d, xg.at[g, slot[0]], xg.at[g, slot[3 if d == 0 else 1]], own_send.at[d, g], own_recv.at[d, g])

    def fwd_copy(d, g):
        cut = side[1 - d]
        return remote(
            d, xg.at[g, slot[3 if d == 0 else 1], cut], xg.at[g, slot[2], cut], fwd_send.at[d, g], fwd_recv.at[d, g]
        )

    def p_copy(d, h, c):
        return remote(d, pout.at[d, c], pin.at[d, h * chunks + c], p_send.at[d, c], p_recv.at[d, h * chunks + c])

    def q_copy(d, h, c):
        return remote(d, qout.at[d, c], qin.at[d, h * chunks + c], q_send.at[d, c], q_recv.at[d, h * chunks + c])

    def w_copies(g):
        s, c = g % 2, g % chunks
        piece = pl.ds(pl.multiple_of(c * KC, KC), KC)
        return [pltpu.make_async_copy(w.at[piece], wgu.at[s, i], w_sem.at[s, i]) for i, w in enumerate((wg, wu))]

    def wd_copy(g):
        s, c = g % 2, g % chunks
        return pltpu.make_async_copy(wd.at[:, pl.ds(pl.multiple_of(c * KC, KC), KC)], wdb.at[s], wd_sem.at[s])

    def y_copy(g):
        h, c = g // chunks, g % chunks
        return pltpu.make_async_copy(
            yst.at[g],
            y.at[pl.ds(pl.multiple_of(h * part, part), part), pl.ds(pl.multiple_of(c * KC, KC), KC)],
            y_sem.at[g],
        )

    def each(count, f):
        def body(i, carry):
            f(i)
            return carry

        lax.fori_loop(0, count, body, 0)

    def start_own(g):
        load(g).wait()
        for d in range(2):
            own_copy(d, g).start()

    def forward(g):
        for d in range(2):
            own_copy(d, g).wait_recv()
            fwd_copy(d, g).start()
        when(g + AHEAD < total, lambda: start_own(g + AHEAD))

    def gate_up(g, first, last):
        s = g % 2
        for copy in w_copies(g):
            copy.wait()

        def tile(j):
            cut = pl.ds(pl.multiple_of(j * NT, NT), NT)
            block = xg[g]
            gate = jnp.dot(block, wgu[s, 0, :, cut], preferred_element_type=jnp.float32)
            if not first:
                gate += accg[:, cut]
            if not last:
                accg[:, cut] = gate
            up = jnp.dot(block, wgu[s, 1, :, cut], preferred_element_type=jnp.float32)
            if not first:
                up += accu[:, cut]
            if not last:
                accu[:, cut] = up
            else:
                hid[:, cut] = (jax.nn.silu(gate) * up).astype(hid.dtype)

        each(hidden // NT, tile)

        def prefetch():
            for copy in w_copies(g + 2):
                copy.start()

        when(g + 2 < total, prefetch)

    def gather_phase(h, before):
        def step(c, first, last):
            g = h * chunks + c
            before(c)
            for d in range(2):
                fwd_copy(d, g).wait_recv()
            gate_up(g, first, last)

        step(0, True, False)
        each(chunks - 2, lambda i: step(i + 1, False, False))
        step(chunks - 1, False, True)

    def down(h, c):
        g = h * chunks + c
        s = g % 2
        wd_copy(g).wait()
        if h:
            for d in range(2):
                p_copy(d, h - 1, c).wait_send()
        term = jnp.dot(hid[...], wdb[s], preferred_element_type=jnp.float32)
        mine = [term[i * part : (i + 1) * part] for i in range(n)]
        for d in range(2):
            near = mine[1 if d == 0 else 3]
            lo = slice(d * half, (d + 1) * half)
            hi = slice((1 - d) * half, (2 - d) * half)
            pout[d, c, 0] = mine[2][:, lo].astype(pout.dtype)
            pout[d, c, 1] = near[:, hi].astype(pout.dtype)
            tq[d, c] = near[:, lo]
        own[g] = mine[0]
        when(g + 2 < total, lambda: wd_copy(g + 2).start())

    def send_p(h, c):
        for d in range(2):
            p_copy(d, h, c).start()

    def sum_q(h, c):
        g = h * chunks + c
        for d in range(2):
            p_copy(d, h, c).wait_recv()
            if h:
                q_copy(d, h - 1, c).wait_send()
            qout[d, c] = (tq[d, c] + pin[d, g, 0].astype(jnp.float32)).astype(qout.dtype)

    def send_q(h, c):
        for d in range(2):
            q_copy(d, h, c).start()

    def finish(h, c):
        g = h * chunks + c
        for d in range(2):
            q_copy(d, h, c).wait_recv()
        for d in range(2):
            cut = side[d]
            out = own[g, :, cut] + qin[d, g].astype(jnp.float32) + pin[1 - d, g, 1].astype(jnp.float32)
            yst[g, :, cut] = out.astype(yst.dtype)
        y_copy(g).start()

    load(0).start()
    for copy in w_copies(0):
        copy.start()
    each(total - 1, lambda i: load(i + 1).start())
    for copy in w_copies(1):
        copy.start()
    for g in range(2):
        wd_copy(g).start()
    barrier = pltpu.get_barrier_semaphore()
    for neighbour in target:
        pl.semaphore_signal(barrier, inc=1, device_id={"tp": neighbour}, device_id_type=pl.DeviceIdType.MESH)
    pl.semaphore_wait(barrier, 2)

    for g in range(AHEAD):
        start_own(g)
    forward(0)

    gather_phase(0, lambda c: forward(c + 1))

    def down0(c):
        when(c % 2 == 0, lambda: forward(chunks + 1 + c // 2))
        down(0, c)

    each(chunks, down0)

    passed = chunks + 1 + (chunks + 1) // 2

    def before1(c):
        when(passed + c < total, lambda: forward(passed + c))
        for k in range(2):
            i = 2 * (c - 2) + k
            when((i >= 0) & (i < chunks) if not isinstance(i, int) else 0 <= i < chunks, lambda i=i: send_p(0, i))
        for k in range(2):
            i = 2 * (c - 7) + k
            ok = (i >= 0) & (i < chunks) if not isinstance(i, int) else 0 <= i < chunks

            def pair(i=i):
                sum_q(0, i)
                send_q(0, i)

            when(ok, pair)

    gather_phase(1, before1)

    summed = 2 * (chunks - 7)

    def down1(c):
        when(summed + c < chunks, lambda: sum_q(0, summed + c))
        down(1, c)
        when(summed + c < chunks, lambda: send_q(0, summed + c))
        send_p(1, c)

    each(chunks, down1)

    def tail(c):
        sum_q(1, c)
        finish(0, c)
        send_q(1, c)

    each(chunks, tail)
    each(chunks, lambda c: finish(1, c))

    def drain(g):
        for d in range(2):
            own_copy(d, g).wait_send()
            fwd_copy(d, g).wait_send()
        y_copy(g).wait()

    each(total, drain)

    def drain_sums(c):
        for d in range(2):
            p_copy(d, 1, c).wait_send()
            q_copy(d, 1, c).wait_send()

    each(chunks, drain_sums)


def solution(mesh):
    n = mesh.shape["tp"]

    def step(x, w_gate, w_up, w_down):
        rows, cols = x.shape
        hidden = w_gate.shape[1]
        part = rows // HALVES
        chunks = cols // KC
        total = HALVES * chunks
        half = KC // 2
        assert n == 4 and rows % HALVES == 0 and cols % KC == 0 and chunks % 2 == 0
        f32, b16 = jnp.float32, x.dtype
        return pl.pallas_call(
            functools.partial(kernel, n),
            out_shape=jax.ShapeDtypeStruct((rows, cols), b16),
            in_specs=[pl.BlockSpec(memory_space=pl.ANY)] * 4,
            out_specs=pl.BlockSpec(memory_space=pl.ANY),
            scratch_shapes=[
                pltpu.VMEM((total, n * part, KC), b16),
                pltpu.VMEM((n * part, hidden), f32),
                pltpu.VMEM((n * part, hidden), f32),
                pltpu.VMEM((n * part, hidden), b16),
                pltpu.VMEM((2, 2, KC, hidden), b16),
                pltpu.VMEM((2, hidden, KC), b16),
                pltpu.VMEM((2, chunks, 2, part, half), b16),
                pltpu.VMEM((2, total, 2, part, half), b16),
                pltpu.VMEM((2, chunks, part, half), b16),
                pltpu.VMEM((2, total, part, half), b16),
                pltpu.VMEM((2, chunks, part, half), f32),
                pltpu.VMEM((total, part, KC), f32),
                pltpu.VMEM((total, part, KC), b16),
                pltpu.SemaphoreType.DMA((total,)),
                pltpu.SemaphoreType.DMA((2, 2)),
                pltpu.SemaphoreType.DMA((2,)),
                pltpu.SemaphoreType.DMA((2, total)),
                pltpu.SemaphoreType.DMA((2, total)),
                pltpu.SemaphoreType.DMA((2, total)),
                pltpu.SemaphoreType.DMA((2, total)),
                pltpu.SemaphoreType.DMA((2, chunks)),
                pltpu.SemaphoreType.DMA((2, total)),
                pltpu.SemaphoreType.DMA((2, chunks)),
                pltpu.SemaphoreType.DMA((2, total)),
                pltpu.SemaphoreType.DMA((total,)),
            ],
            compiler_params=pltpu.CompilerParams(
                collective_id=0, has_side_effects=True, vmem_limit_bytes=67043328
            ),
            name="mlp_ring",
        )(x, w_gate, w_up, w_down)

    return jax.shard_map(
        step,
        mesh=mesh,
        in_specs=(P(("dp", "tp"), None), P(None, "tp"), P(None, "tp"), P("tp", None)),
        out_specs=P(("dp", "tp"), None),
        check_vma=False,
    )
```

time: 292 us -> 161 us (0.55)
  waiting for transfers between devices: 175 us -> 0 us
  Pallas kernels: 0 us -> 158 us
  matrix products: 103 us -> 0 us
  between operations: 13.4 us -> 0.01 us
  local copies, waits for them, and re-layouts: 0.01 us -> 3.18 us
    pallas_call x0 -> x1, Pallas kernels: none -> 158 us  [step(): pl.pallas_call(functools.partial(kernel, n), out_shape=jax.ShapeDtypeStru...]
    dot_general x3 -> x0, matrix products: 103 us -> none  [the longest x1 35 us: step(): jnp.dot(hidden, w_down, preferred_element_type=jnp.float32)]
    all_gather x1 -> x0, waiting for transfers between devices: 90.4 us -> none  [step(): rows = lax.all_gather(x, 'tp', axis=0, tiled=True)]
    reduce_scatter x1 -> x0, waiting for transfers between devices: 83.9 us -> none  [step(): return lax.psum_scatter(term, 'tp', scatter_dimension=0, tiled=True)]
    unnamed x2 -> x1, local copies, waits for them, and re-layouts: 0.01 us -> 3.18 us
  transfers between devices with their start and end apart: 2 -> 0, of which waited for: 2 -> 0; matrix products, arithmetic and copies ran while one was open for 0% -> 0% of each run, Pallas kernels for 0% -> 0%
where the time goes in v1:
time: 161 us
  Pallas kernels  158 us (98%)
  local copies, waits for them, and re-layouts  3.18 us (2%)
    pallas_call x1, Pallas kernels, step(): pl.pallas_call(functools.partial(kernel, n), out_shape=jax.ShapeDtypeStru...  158 us

profile of v1, /device:TPU:112, one launch (start us, length us, event | category | flops | bytes accessed | tf_op | source)
XLA Modules:
  0.0 160.9 jit_solution(7425521337878358358)
XLA Ops:
  0.0 157.7 %mlp_ring.1 = bf16[224,5120]{1,0:T(8,128)(2,1)} custom-call(bf16[224,5120]{1,0:T(8,128)(2,1)} %x.1, bf16[5120,3072]{1,0:T(8,128)(2,1)} %wg.1, bf16[5120,3072]{1,0:T(8,128)(2,1)} %wu.1, bf16[3072,5120]{1,0:T(8,128)(2,1)} %wd.1), custom_call_target="tpu_custom_call" | custom-call | tf_op jit(solution)/shard_map/mlp_ring/pallas_call | solution.py:282
  157.7 3.2 %copy.6 = bf16[224,5120]{1,0:T(8,128)(2,1)} copy(bf16[224,5120]{1,0:T(8,128)(2,1)} %mlp_ring.1) | data formatting | bytes 4587520

commit v2 on v1

v2 whole, which is shorter than its diff:
```python
import functools

import jax
import jax.numpy as jnp
from jax import lax
from jax.experimental import pallas as pl
from jax.experimental.pallas import tpu as pltpu
from jax.sharding import PartitionSpec as P

HALVES = 2
KC = 1024
KT = KC // 2
NT = 1536
AHEAD = 2
PLAN = (
    {(0, 0): [("f", 1)], (0, 1): [("f", 2)], (2, 0): [("f", 3)], (3, 0): [("f", 4)], (4, 0): [("f", 5)]},
    {(0, 0): [("f", 6)], (1, 1): [("p", 0)], (3, 0): [("f", 7)]},
    {(0, 0): [("p", 1), ("q", 0)], (1, 0): [("f", 8)], (1, 1): [("p", 2)], (2, 0): [("f", 9)], (2, 1): [("p", 3)], (3, 0): [("q", 1)], (3, 1): [("p", 4), ("q", 2)]},
    {(0, 0): [("q", 3)], (0, 1): [("q", 4)]},
)


def when(cond, f):
    if isinstance(cond, bool):
        if cond:
            f()
    else:
        pl.when(cond)(f)


def kernel(
    n, x, wg, wu, wd, y,
    xg, accg, accu, hid, wgu, wdb, pout, pin, qout, qin, tq, own,
    ld_sem, w_sem, wd_sem, own_send, own_recv, fwd_send, fwd_recv,
    p_send, p_recv, q_send, q_recv,
):
    me = lax.axis_index("tp")
    right, left = lax.rem(me + 1, n), lax.rem(me + n - 1, n)
    target = (right, left)
    rows, cols = x.shape
    part = rows // HALVES
    chunks = cols // KC
    total = HALVES * chunks
    hidden = wg.shape[1]
    half = KC // 2
    slot = [pl.ds(i * part, part) for i in range(n)]
    side = (pl.ds(0, half), pl.ds(half, half))

    def load(g):
        h, c = g // chunks, g % chunks
        return pltpu.make_async_copy(
            x.at[pl.ds(pl.multiple_of(h * part, part), part), pl.ds(pl.multiple_of(c * KC, KC), KC)],
            xg.at[g, slot[0]],
            ld_sem.at[g],
        )

    def remote(d, src, dst, send, recv):
        return pltpu.make_async_remote_copy(
            src_ref=src, dst_ref=dst, send_sem=send, recv_sem=recv,
            device_id={"tp": target[d]}, device_id_type=pl.DeviceIdType.MESH,
        )

    def own_copy(d, g):
        return remote(d, xg.at[g, slot[0]], xg.at[g, slot[3 if d == 0 else 1]], own_send.at[d, g], own_recv.at[d, g])

    def fwd_copy(d, g):
        cut = side[1 - d]
        return remote(
            d, xg.at[g, slot[3 if d == 0 else 1], cut], xg.at[g, slot[2], cut], fwd_send.at[d, g], fwd_recv.at[d, g]
        )

    def p_copy(d, h, c):
        return remote(d, pout.at[d, c], pin.at[d, h * chunks + c], p_send.at[d, c], p_recv.at[d, h * chunks + c])

    def q_copy(d, h, c):
        return remote(d, qout.at[d, c], qin.at[d, h * chunks + c], q_send.at[d, c], q_recv.at[d, h * chunks + c])

    tiles = 2 * chunks

    wide = hidden // 2

    def w_copies(g, s):
        piece = pl.ds(pl.multiple_of(g % chunks * KC, KC), KC), pl.ds(s * wide, wide)
        return [pltpu.make_async_copy(w.at[piece], wgu.at[s, k], w_sem.at[s, k]) for k, w in enumerate((wg, wu))]

    def wd_copy(i):
        s, piece = i % 2, pl.ds(pl.multiple_of(i % tiles * KT, KT), KT)
        return pltpu.make_async_copy(wd.at[:, piece], wdb.at[s], wd_sem.at[s])

    def each(count, f):
        def body(i, carry):
            f(i)
            return carry

        lax.fori_loop(0, count, body, 0)

    def start_own(g):
        load(g).wait()
        for d in range(2):
            own_copy(d, g).start()

    def forward(g):
        for d in range(2):
            own_copy(d, g).wait_recv()
            fwd_copy(d, g).start()
        when(g + AHEAD < total, lambda: start_own(g + AHEAD))

    def gate_up(g, s, first, last):
        for copy in w_copies(g, s):
            copy.wait()

        def tile(j):
            w_cut = pl.ds(pl.multiple_of(j * NT, NT), NT)
            cut = pl.ds(pl.multiple_of(s * wide + j * NT, NT), NT)
            block = xg[g]
            gate = jnp.dot(block, wgu[s, 0, :, w_cut], preferred_element_type=jnp.float32)
            if not first:
                gate += accg[:, cut]
            if not last:
                accg[:, cut] = gate
            up = jnp.dot(block, wgu[s, 1, :, w_cut], preferred_element_type=jnp.float32)
            if not first:
                up += accu[:, cut]
            if not last:
                accu[:, cut] = up
            else:
                hid[:, cut] = (jax.nn.silu(gate) * up).astype(hid.dtype)

        each(wide // NT, tile)

        def prefetch():
            for copy in w_copies(g + 1, s):
                copy.start()

        when(g + 1 < total, prefetch)

    def gather_phase(h, before):
        def step(c, first, last):
            g = h * chunks + c
            before(c, 0)
            for d in range(2):
                fwd_copy(d, g).wait_recv()
            gate_up(g, 0, first, last)
            before(c, 1)
            gate_up(g, 1, first, last)

        step(0, True, False)
        each(chunks - 2, lambda i: step(i + 1, False, False))
        step(chunks - 1, False, True)

    def down(h, c, before):
        g = h * chunks + c
        if h:
            for d in range(2):
                p_copy(d, h - 1, c).wait_send()
        for s in range(2):
            before(c, s)
            i = 2 * g + s
            wd_copy(i).wait()
            term = jnp.dot(hid[...], wdb[s], preferred_element_type=jnp.float32)
            mine, near, far, last = [term[k * part : (k + 1) * part] for k in range(n)]
            if s:
                near, last = last, near
            pout[s, c, 0] = far.astype(pout.dtype)
            tq[s, c] = near
            pout[1 - s, c, 1] = last.astype(pout.dtype)
            own[g, :, side[s]] = mine
            when(i + 2 < 2 * total, lambda: wd_copy(i + 2).start())

    def send_p(h, c):
        for d in range(2):
            p_copy(d, h, c).start()

    def sum_q(h, c):
        g = h * chunks + c
        for d in range(2):
            p_copy(d, h, c).wait_recv()
            if h:
                q_copy(d, h - 1, c).wait_send()
            qout[d, c] = (tq[d, c] + pin[d, g, 0].astype(jnp.float32)).astype(qout.dtype)
        for d in range(2):
            own[g, :, side[d]] += pin[1 - d, g, 1].astype(jnp.float32)

    def send_q(h, c):
        for d in range(2):
            q_copy(d, h, c).start()

    def finish(h, c):
        g = h * chunks + c
        for d in range(2):
            q_copy(d, h, c).wait_recv()
            y[
                pl.ds(pl.multiple_of(h * part, part), part), pl.ds(pl.multiple_of(c * KC + d * half, half), half)
            ] = (own[g, :, side[d]] + qin[d, g].astype(jnp.float32)).astype(y.dtype)

    barrier = pltpu.get_barrier_semaphore()
    for neighbour in target:
        pl.semaphore_signal(barrier, inc=1, device_id={"tp": neighbour}, device_id_type=pl.DeviceIdType.MESH)
    for g in range(AHEAD):
        load(g).start()
    pl.semaphore_wait(barrier, 2)
    for g in range(AHEAD):
        start_own(g)
    for s in range(2):
        for copy in w_copies(0, s):
            copy.start()
    each(total - AHEAD, lambda i: load(i + AHEAD).start())
    for i in range(2):
        wd_copy(i).start()
    forward(0)

    def send_sum(c):
        sum_q(0, c)
        send_q(0, c)

    acts = {"f": forward, "p": lambda c: send_p(0, c), "q": send_sum}

    def slots(phase):
        def before(c, s):
            for (k, t), todo in PLAN[phase].items():
                if t == s and (not isinstance(c, int) or c == k):

                    def go(todo=todo):
                        for name, i in todo:
                            acts[name](i)

                    when(c == k, go)

        return before

    gather_phase(0, slots(0))
    each(chunks, lambda c: down(0, c, slots(1)))
    gather_phase(1, slots(2))

    def down1(c):
        down(1, c, slots(3))
        send_p(1, c)

    each(chunks, down1)

    def tail(c):
        sum_q(1, c)
        finish(0, c)
        send_q(1, c)

    each(chunks, tail)

    def drain(g):
        for d in range(2):
            own_copy(d, g).wait_send()
            fwd_copy(d, g).wait_send()

    each(total, drain)

    def drain_sums(c):
        for d in range(2):
            p_copy(d, 1, c).wait_send()

    each(chunks, drain_sums)

    def end(c):
        finish(1, c)
        for d in range(2):
            q_copy(d, 1, c).wait_send()

    each(chunks, end)


def solution(mesh):
    n = mesh.shape["tp"]

    def step(x, w_gate, w_up, w_down):
        rows, cols = x.shape
        hidden = w_gate.shape[1]
        part = rows // HALVES
        chunks = cols // KC
        total = HALVES * chunks
        half = KC // 2
        assert n == 4 and HALVES == 2 and rows % HALVES == 0 and cols % KC == 0 and 2 * chunks == 1 + sum(k == "f" for p in PLAN for todo in p.values() for k, _ in todo)
        f32, b16 = jnp.float32, x.dtype
        return pl.pallas_call(
            functools.partial(kernel, n),
            out_shape=pltpu.VMEM((rows, cols), b16),
            in_specs=[pl.BlockSpec(memory_space=pl.ANY)] * 4,
            out_specs=pl.BlockSpec(memory_space=pltpu.VMEM),
            scratch_shapes=[
                pltpu.VMEM((total, n * part, KC), b16),
                pltpu.VMEM((n * part, hidden), f32),
                pltpu.VMEM((n * part, hidden), f32),
                pltpu.VMEM((n * part, hidden), b16),
                pltpu.VMEM((2, 2, KC, hidden // 2), b16),
                pltpu.VMEM((2, hidden, KT), b16),
                pltpu.VMEM((2, chunks, 2, part, half), b16),
                pltpu.VMEM((2, total, 2, part, half), b16),
                pltpu.VMEM((2, chunks, part, half), b16),
                pltpu.VMEM((2, total, part, half), b16),
                pltpu.VMEM((2, chunks, part, half), f32),
                pltpu.VMEM((total, part, KC), f32),
                pltpu.SemaphoreType.DMA((total,)),
                pltpu.SemaphoreType.DMA((2, 2)),
                pltpu.SemaphoreType.DMA((2,)),
                pltpu.SemaphoreType.DMA((2, total)),
                pltpu.SemaphoreType.DMA((2, total)),
                pltpu.SemaphoreType.DMA((2, total)),
                pltpu.SemaphoreType.DMA((2, total)),
                pltpu.SemaphoreType.DMA((2, chunks)),
                pltpu.SemaphoreType.DMA((2, total)),
                pltpu.SemaphoreType.DMA((2, chunks)),
                pltpu.SemaphoreType.DMA((2, total)),
            ],
            compiler_params=pltpu.CompilerParams(
                collective_id=0, has_side_effects=True, vmem_limit_bytes=64_700_000
            ),
            name="mlp_ring",
        )(x, w_gate, w_up, w_down)

    return jax.shard_map(
        step,
        mesh=mesh,
        in_specs=(P(("dp", "tp"), None), P(None, "tp"), P(None, "tp"), P("tp", None)),
        out_specs=P(("dp", "tp"), None),
        check_vma=False,
    )
```

time: 161 us -> 156 us (0.969)
  Pallas kernels: 158 us -> 154 us
  local copies, waits for them, and re-layouts: 3.18 us -> 1.39 us
    pallas_call x1, Pallas kernels: 158 us -> 154 us  [step(): pl.pallas_call(functools.partial(kernel, n), out_shape=pltpu.VMEM((rows,...]
    unnamed x1, local copies, waits for them, and re-layouts: 3.18 us -> 1.39 us
where the time goes in v2:
time: 156 us
  Pallas kernels  154 us (99%)
    pallas_call x1, Pallas kernels, step(): pl.pallas_call(functools.partial(kernel, n), out_shape=pltpu.VMEM((rows,...  154 us

profile of v2, /device:TPU:112, one launch (start us, length us, event | category | flops | bytes accessed | tf_op | source)
XLA Modules:
  0.0 155.9 jit_solution(8945067862857011296)
XLA Ops:
  0.0 154.5 %mlp_ring.1 = bf16[224,5120]{1,0:T(8,128)(2,1)S(1)} custom-call(bf16[224,5120]{1,0:T(8,128)(2,1)} %x.1, bf16[5120,3072]{1,0:T(8,128)(2,1)} %wg.1, bf16[5120,3072]{1,0:T(8,128)(2,1)} %wu.1, bf16[3072,5120]{1,0:T(8,128)(2,1)} %wd.1), custom_call_target="tpu_custom_call" | custom-call | tf_op jit(solution)/shard_map/mlp_ring/pallas_call | solution.py:281
  154.5 1.4 copy.6

commit v3 on v2

--- a/solution.py
+++ b/solution.py
@@ -11,12 +11,14 @@
 KC = 1024
 KT = KC // 2
 NT = 1536
+GATHER = ((0, 1), (1, 1), (2, 1), (3, 1), (4, 1), (5, 2), (7, 3))
+SUMS = (((0, 2), (2, 3)), ((0, 1), (1, 1), (2, 1), (3, 1), (4, 1)))
 AHEAD = 2
 PLAN = (
-    {(0, 0): [("f", 1)], (0, 1): [("f", 2)], (2, 0): [("f", 3)], (3, 0): [("f", 4)], (4, 0): [("f", 5)]},
-    {(0, 0): [("f", 6)], (1, 1): [("p", 0)], (3, 0): [("f", 7)]},
-    {(0, 0): [("p", 1), ("q", 0)], (1, 0): [("f", 8)], (1, 1): [("p", 2)], (2, 0): [("f", 9)], (2, 1): [("p", 3)], (3, 0): [("q", 1)], (3, 1): [("p", 4), ("q", 2)]},
-    {(0, 0): [("q", 3)], (0, 1): [("q", 4)]},
+    {(0, 0): [("o", 2), ("f", 1)], (0, 1): [("o", 3), ("f", 2)], (1, 0): [("o", 4)], (2, 0): [("f", 3)], (2, 1): [("f", 4), ("o", 5), ("o", 6)]},
+    {(0, 1): [("f", 5)], (3, 1): [("f", 6)], (4, 1): [("p", 0)]},
+    {(0, 1): [("p", 1)], (3, 0): [("q", 0)], (4, 1): [("q", 1)]},
+    {},
 )
 
 
@@ -60,20 +62,42 @@
             device_id={"tp": target[d]}, device_id_type=pl.DeviceIdType.MESH,
         )
 
-    def own_copy(d, g):
-        return remote(d, xg.at[g, slot[0]], xg.at[g, slot[3 if d == 0 else 1]], own_send.at[d, g], own_recv.at[d, g])
-
-    def fwd_copy(d, g):
-        cut = side[1 - d]
+    def own_copy(d, j):
+        a = pl.ds(*GATHER[j])
+        src = x.at[slot[0], pl.ds(0, KC)] if j == 0 else xg.at[a, slot[0]]
+        dst = xg.at[0 if j == 0 else a, slot[3 if d == 0 else 1]]
+        return remote(d, src, dst, own_send.at[d, j], own_recv.at[d, j])
+
+    def fwd_copy(d, j):
+        a, cut = pl.ds(*GATHER[j]), side[1 - d]
         return remote(
-            d, xg.at[g, slot[3 if d == 0 else 1], cut], xg.at[g, slot[2], cut], fwd_send.at[d, g], fwd_recv.at[d, g]
+            d, xg.at[a, slot[3 if d == 0 else 1], cut], xg.at[a, slot[2], cut], fwd_send.at[d, j], fwd_recv.at[d, j]
         )
 
-    def p_copy(d, h, c):
-        return remote(d, pout.at[d, c], pin.at[d, h * chunks + c], p_send.at[d, c], p_recv.at[d, h * chunks + c])
-
-    def q_copy(d, h, c):
-        return remote(d, qout.at[d, c], qin.at[d, h * chunks + c], q_send.at[d, c], q_recv.at[d, h * chunks + c])
+    def sum_copy(d, h, j, src, dst, send, recv):
+        a, k = SUMS[h][j]
+        t = j + h * len(SUMS[0])
+        return remote(
+            d, src.at[d, pl.ds(a, k)], dst.at[d, pl.ds(h * chunks + a, k)], send.at[d, t], recv.at[d, t]
+        )
+
+    def p_copy(d, h, j):
+        return sum_copy(d, h, j, pout, pin, p_send, p_recv)
+
+    def q_copy(d, h, j):
+        return sum_copy(d, h, j, qout, qin, q_send, q_recv)
+
+    def both(f):
+        for d in range(2):
+            f(d)
+
+    def at_first(groups, c, f):
+        for j, (a, _) in enumerate(groups):
+            when(c == a, lambda j=j: f(j))
+
+    def at_last(groups, c, f):
+        for j, (a, k) in enumerate(groups):
+            when(c == a + k - 1, lambda j=j: f(j))
 
     tiles = 2 * chunks
 
@@ -94,16 +118,17 @@
 
         lax.fori_loop(0, count, body, 0)
 
-    def start_own(g):
-        load(g).wait()
-        for d in range(2):
-            own_copy(d, g).start()
-
-    def forward(g):
-        for d in range(2):
-            own_copy(d, g).wait_recv()
-            fwd_copy(d, g).start()
-        when(g + AHEAD < total, lambda: start_own(g + AHEAD))
+    def start_own(j):
+        a, k = GATHER[j]
+        if j:
+            for g in range(a, a + k):
+                load(g).wait()
+        both(lambda d: own_copy(d, j).start())
+
+    def forward(j):
+        for d in range(2):
+            own_copy(d, j).wait_recv()
+            fwd_copy(d, j).start()
 
     def gate_up(g, s, first, last):
         for copy in w_copies(g, s):
@@ -138,8 +163,9 @@
         def step(c, first, last):
             g = h * chunks + c
             before(c, 0)
-            for d in range(2):
-                fwd_copy(d, g).wait_recv()
+            for j, (a, _) in enumerate(GATHER):
+                if a // chunks == h:
+                    when(c == a - h * chunks, lambda j=j: both(lambda d: fwd_copy(d, j).wait_recv()))
             gate_up(g, 0, first, last)
             before(c, 1)
             gate_up(g, 1, first, last)
@@ -151,8 +177,7 @@
     def down(h, c, before):
         g = h * chunks + c
         if h:
-            for d in range(2):
-                p_copy(d, h - 1, c).wait_send()
+            at_first(SUMS[0], c, lambda j: both(lambda d: p_copy(d, 0, j).wait_send()))
         for s in range(2):
             before(c, s)
             i = 2 * g + s
@@ -167,28 +192,16 @@
             own[g, :, side[s]] = mine
             when(i + 2 < 2 * total, lambda: wd_copy(i + 2).start())
 
-    def send_p(h, c):
-        for d in range(2):
-            p_copy(d, h, c).start()
-
-    def sum_q(h, c):
+    def add(h, c):
         g = h * chunks + c
         for d in range(2):
-            p_copy(d, h, c).wait_recv()
-            if h:
-                q_copy(d, h - 1, c).wait_send()
             qout[d, c] = (tq[d, c] + pin[d, g, 0].astype(jnp.float32)).astype(qout.dtype)
         for d in range(2):
             own[g, :, side[d]] += pin[1 - d, g, 1].astype(jnp.float32)
-
-    def send_q(h, c):
-        for d in range(2):
-            q_copy(d, h, c).start()
 
     def finish(h, c):
         g = h * chunks + c
         for d in range(2):
-            q_copy(d, h, c).wait_recv()
             y[
                 pl.ds(pl.multiple_of(h * part, part), part), pl.ds(pl.multiple_of(c * KC + d * half, half), half)
             ] = (own[g, :, side[d]] + qin[d, g].astype(jnp.float32)).astype(y.dtype)
@@ -199,21 +212,27 @@
     for g in range(AHEAD):
         load(g).start()
     pl.semaphore_wait(barrier, 2)
-    for g in range(AHEAD):
-        start_own(g)
+    for j in range(AHEAD):
+        start_own(j)
     for s in range(2):
         for copy in w_copies(0, s):
             copy.start()
     each(total - AHEAD, lambda i: load(i + AHEAD).start())
     for i in range(2):
         wd_copy(i).start()
+    load(0).wait()
     forward(0)
 
-    def send_sum(c):
-        sum_q(0, c)
-        send_q(0, c)
-
-    acts = {"f": forward, "p": lambda c: send_p(0, c), "q": send_sum}
+    def send_terms(j):
+        both(lambda d: p_copy(d, 0, j).start())
+
+    def send_sums(j):
+        a, k = SUMS[0][j]
+        both(lambda d: p_copy(d, 0, j).wait_recv())
+        each(k, lambda i: add(0, a + i))
+        both(lambda d: q_copy(d, 0, j).start())
+
+    acts = {"o": start_own, "f": forward, "p": send_terms, "q": send_sums}
 
     def slots(phase):
         def before(c, s):
@@ -221,8 +240,8 @@
                 if t == s and (not isinstance(c, int) or c == k):
 
                     def go(todo=todo):
-                        for name, i in todo:
-                            acts[name](i)
+                        for name, j in todo:
+                            acts[name](j)
 
                     when(c == k, go)
 
@@ -234,34 +253,28 @@
 
     def down1(c):
         down(1, c, slots(3))
-        send_p(1, c)
+        at_last(SUMS[1], c, lambda j: both(lambda d: p_copy(d, 1, j).start()))
 
     each(chunks, down1)
 
     def tail(c):
-        sum_q(1, c)
+        at_first(SUMS[1], c, lambda j: both(lambda d: p_copy(d, 1, j).wait_recv()))
+        at_first(SUMS[0], c, lambda j: both(lambda d: q_copy(d, 0, j).wait()))
+        add(1, c)
         finish(0, c)
-        send_q(1, c)
+        at_last(SUMS[1], c, lambda j: both(lambda d: q_copy(d, 1, j).start()))
 
     each(chunks, tail)
-
-    def drain(g):
-        for d in range(2):
-            own_copy(d, g).wait_send()
-            fwd_copy(d, g).wait_send()
-
-    each(total, drain)
-
-    def drain_sums(c):
-        for d in range(2):
-            p_copy(d, 1, c).wait_send()
-
-    each(chunks, drain_sums)
+    for d in range(2):
+        for j in range(len(GATHER)):
+            own_copy(d, j).wait_send()
+            fwd_copy(d, j).wait_send()
+        for j in range(len(SUMS[1])):
+            p_copy(d, 1, j).wait_send()
 
     def end(c):
+        at_first(SUMS[1], c, lambda j: both(lambda d: q_copy(d, 1, j).wait()))
         finish(1, c)
-        for d in range(2):
-            q_copy(d, 1, c).wait_send()
 
     each(chunks, end)
 
@@ -276,7 +289,10 @@
         chunks = cols // KC
         total = HALVES * chunks
         half = KC // 2
-        assert n == 4 and HALVES == 2 and rows % HALVES == 0 and cols % KC == 0 and 2 * chunks == 1 + sum(k == "f" for p in PLAN for todo in p.values() for k, _ in todo)
+        assert n == 4 and rows % HALVES == 0 and cols % KC == 0
+        assert GATHER[0] == (0, 1) and GATHER[AHEAD - 1][0] < chunks and sum(k for _, k in GATHER) == total
+        assert len(SUMS) == HALVES and all(sum(k for _, k in groups) == chunks for groups in SUMS)
+        sums = sum(len(groups) for groups in SUMS)
         f32, b16 = jnp.float32, x.dtype
         return pl.pallas_call(
             functools.partial(kernel, n),
@@ -299,14 +315,14 @@
                 pltpu.SemaphoreType.DMA((total,)),
                 pltpu.SemaphoreType.DMA((2, 2)),
                 pltpu.SemaphoreType.DMA((2,)),
-                pltpu.SemaphoreType.DMA((2, total)),
-                pltpu.SemaphoreType.DMA((2, total)),
-                pltpu.SemaphoreType.DMA((2, total)),
-                pltpu.SemaphoreType.DMA((2, total)),
-                pltpu.SemaphoreType.DMA((2, chunks)),
-                pltpu.SemaphoreType.DMA((2, total)),
-                pltpu.SemaphoreType.DMA((2, chunks)),
-                pltpu.SemaphoreType.DMA((2, total)),
+                pltpu.SemaphoreType.DMA((2, len(GATHER))),
+                pltpu.SemaphoreType.DMA((2, len(GATHER))),
+                pltpu.SemaphoreType.DMA((2, len(GATHER))),
+                pltpu.SemaphoreType.DMA((2, len(GATHER))),
+                pltpu.SemaphoreType.DMA((2, sums)),
+                pltpu.SemaphoreType.DMA((2, sums)),
+                pltpu.SemaphoreType.DMA((2, sums)),
+                pltpu.SemaphoreType.DMA((2, sums)),
             ],
             compiler_params=pltpu.CompilerParams(
                 collective_id=0, has_side_effects=True, vmem_limit_bytes=64_700_000

time: 156 us -> 155 us (level)
  no operation moved by 1% of the time
where the time goes in v3:
time: 155 us
  Pallas kernels  154 us (99%)
    pallas_call x1, Pallas kernels, step(): pl.pallas_call(functools.partial(kernel, n), out_shape=pltpu.VMEM((rows,...  154 us

profile of v3, /device:TPU:112, one launch (start us, length us, event | category | flops | bytes accessed | tf_op | source)
XLA Modules:
  0.0 155.1 jit_solution(185583590960732075)
XLA Ops:
  0.0 153.7 %mlp_ring.1 = bf16[224,5120]{1,0:T(8,128)(2,1)S(1)} custom-call(bf16[224,5120]{1,0:T(8,128)(2,1)} %x.1, bf16[5120,3072]{1,0:T(8,128)(2,1)} %wg.1, bf16[5120,3072]{1,0:T(8,128)(2,1)} %wu.1, bf16[3072,5120]{1,0:T(8,128)(2,1)} %wd.1), custom_call_target="tpu_custom_call" | custom-call | tf_op jit(solution)/shard_map/mlp_ring/pallas_call | solution.py:297
  153.7 1.4 copy.6
